TPU v7x, 32 devices: a whole 2x2x4 slice. The times are simulated.
32 devices in a mesh: group: 8 (over y, x, core), head: 4 (over z).
Axes of the slice: x: 2, y: 2, z: 4, core: 2. Of those that a mesh axis runs over, the one named last changes fastest.
Arguments:
- hidden_in: bfloat16 [128, 2560], P('group'), may hold values from -6 to 6
- ssm_state: float32 [128, 80, 64, 128], P('group', 'head'), may hold values from -6 to 6
- conv_x_state: bfloat16 [128, 3, 5120], P('group', None, 'head'), may hold values from -6 to 6
- conv_bc_state: bfloat16 [128, 3, 256], P('group'), may hold values from -6 to 6
- token_ids: int32 [128], P('group'), may hold values from 0 to 25599
- ref_logits: bfloat16 [128, 25600], P('group', 'head'), may hold values from -15 to 350
- in_z: bfloat16 [2560, 5120], P('group', 'head'), may hold values from -0.125 to 0.125
- in_x: bfloat16 [2560, 5120], P('group', 'head'), may hold values from -0.125 to 0.125
- in_bc: bfloat16 [2560, 256], P('group'), may hold values from -0.125 to 0.125
- in_dt: bfloat16 [2560, 80], P('group', 'head'), may hold values from -0.125 to 0.125
- out_t: bfloat16 [2560, 5120], P('group', 'head'), may hold values from -0.078125 to 0.078125
- lm_head: bfloat16 [25600, 2560], P('head', 'group'), may hold values from -6 to 6
- conv_wx: float32 [4, 5120], P(None, 'head'), may hold values from -3 to 3
- conv_bx: float32 [5120], P('head'), may hold values from -1.5 to 1.5
- conv_wbc: float32 [4, 256], replicated, may hold values from -3 to 3
- conv_bbc: float32 [256], replicated, may hold values from -1.5 to 1.5
- dt_bias: float32 [80], P('head'), may hold values from -4 to -1
- a_log: float32 [80], P('head'), may hold values from 0 to 2.77
- skip_gain: float32 [80], P('head'), may hold values from 0.5 to 1.5
- norm_in: float32 [2560], replicated, may hold values from 0.5 to 1.5
- norm_gain: float32 [5120], P('head'), may hold values from 0.5 to 1.5
- final_gain: float32 [2560], replicated, may hold values from 0.5 to 1.5
Outputs:
- new_state: float32 [128, 80, 64, 128], P('group', 'head')
- divergence: float32 [128], P('group')
- token_logprob: float32 [128], P('group')
- roll_z: bfloat16 [2560, 5120], P(None, 'head')
- roll_x: bfloat16 [2560, 5120], P(None, 'head')
- roll_bc: bfloat16 [2560, 256], replicated
- roll_dt: bfloat16 [2560, 80], P(None, 'head')
- roll_out: bfloat16 [2560, 5120], P(None, 'head')
All inputs are finite; a program needn't handle non-finite values.
Results may differ from a plain program's by a relative error of at most 0.0102.
Values may be sent and summed in bfloat16 or wider, within the bound.
A program may use at most 128 MiB of HBM per device.

v0:
```python
import jax
import jax.numpy as jnp
from jax import lax
from jax.sharding import PartitionSpec as P

P_SIZE = 64
EPSILON = 1e-05


def rms_norm(values, gain):
    return values * lax.rsqrt(jnp.mean(values * values, axis=-1, keepdims=True) + EPSILON) * gain


def causal_conv(history, newest, taps, offset):
    window = jnp.concatenate([history, newest[:, None, :]], axis=1).astype(jnp.float32)
    return jax.nn.silu(jnp.sum(window * taps[None, :, :], axis=1) + offset)


def shards(
    hidden_in,
    ssm_state,
    conv_x_state,
    conv_bc_state,
    token_ids,
    ref_logits,
    in_z,
    in_x,
    in_bc,
    in_dt,
    out_t,
    lm_head,
    conv_wx,
    conv_bx,
    conv_wbc,
    conv_bbc,
    dt_bias,
    a_log,
    skip_gain,
    norm_in,
    norm_gain,
    final_gain,
):
    roll_z, roll_x, roll_bc, roll_dt, roll_out = (
        lax.all_gather(in_z, "group", axis=0, tiled=True),
        lax.all_gather(in_x, "group", axis=0, tiled=True),
        lax.all_gather(in_bc, "group", axis=0, tiled=True),
        lax.all_gather(in_dt, "group", axis=0, tiled=True),
        lax.all_gather(out_t, "group", axis=0, tiled=True),
    )
    stream_in = hidden_in.astype(jnp.float32)
    normed = rms_norm(stream_in, norm_in).astype(jnp.bfloat16)
    gate_branch = jnp.dot(normed, roll_z, preferred_element_type=jnp.float32).astype(jnp.bfloat16)
    x_branch = jnp.dot(normed, roll_x, preferred_element_type=jnp.float32).astype(jnp.bfloat16)
    bc_branch = jnp.dot(normed, roll_bc, preferred_element_type=jnp.float32).astype(jnp.bfloat16)
    step_raw = jnp.dot(normed, roll_dt, preferred_element_type=jnp.float32).astype(jnp.bfloat16)
    x_conv = causal_conv(conv_x_state, x_branch, conv_wx, conv_bx)
    bc_conv = causal_conv(conv_bc_state, bc_branch, conv_wbc, conv_bbc)
    state_size = bc_conv.shape[1] // 2
    b_vals = bc_conv[:, :state_size]
    c_vals = bc_conv[:, state_size:]
    step = jax.nn.softplus(step_raw.astype(jnp.float32) + dt_bias)
    decay = jnp.exp(-step * jnp.exp(a_log))
    seq_count = x_conv.shape[0]
    local_heads = a_log.shape[0]
    x_heads = x_conv.reshape(seq_count, local_heads, P_SIZE)
    inflow = (step[:, :, None] * x_heads)[:, :, :, None] * b_vals[:, None, None, :]
    new_state = decay[:, :, None, None] * ssm_state + inflow
    ssm_out = jnp.einsum("shpn,sn->shp", new_state, c_vals, precision=lax.Precision.HIGHEST)
    ssm_out = (ssm_out + skip_gain[None, :, None] * x_heads).reshape(
        seq_count, local_heads * P_SIZE
    )
    gated = ssm_out * jax.nn.silu(gate_branch.astype(jnp.float32))
    square_total = lax.psum(jnp.sum(gated * gated, axis=-1), "head")
    inner_width = gated.shape[1] * lax.axis_size("head")
    gated_out = (
        gated * lax.rsqrt(square_total / inner_width + EPSILON)[:, None] * norm_gain
    ).astype(jnp.bfloat16)
    partial_mix = lax.dot_general(
        gated_out, roll_out, (((1,), (1,)), ((), ())), preferred_element_type=jnp.float32
    )
    mixed = lax.psum(partial_mix, "head")
    final_hidden = rms_norm(stream_in + mixed, final_gain).astype(jnp.bfloat16)
    vocab_local = lm_head.shape[0]
    whole_rows = lax.all_to_all(lm_head, "group", split_axis=0, concat_axis=1, tiled=True)
    every_logits = lax.dot_general(
        lax.all_gather(final_hidden, "group", axis=0, tiled=True),
        whole_rows,
        (((1,), (1,)), ((), ())),
        preferred_element_type=jnp.float32,
    )
    logits = lax.all_to_all(every_logits, "group", split_axis=0, concat_axis=1, tiled=True)
    reference_rows = ref_logits.astype(jnp.float32)
    column_ids = lax.axis_index("head") * vocab_local + lax.broadcasted_iota(
        jnp.int32, (1, vocab_local), 1
    )
    picked_part = jnp.sum(jnp.where(column_ids == token_ids[:, None], logits, 0.0), axis=-1)
    roll_max, ref_max = lax.pmax(
        (jnp.max(logits, axis=-1), jnp.max(reference_rows, axis=-1)), "head"
    )
    ref_weights = jnp.exp(reference_rows - ref_max[:, None])
    roll_sum, ref_sum, cross_sum, picked = lax.psum(
        (
            jnp.sum(jnp.exp(logits - roll_max[:, None]), axis=-1),
            jnp.sum(ref_weights, axis=-1),
            jnp.sum(ref_weights * (reference_rows - logits), axis=-1),
            picked_part,
        ),
        "head",
    )
    lse_roll = roll_max + jnp.log(roll_sum)
    lse_ref = ref_max + jnp.log(ref_sum)
    divergence = cross_sum / ref_sum - lse_ref + lse_roll
    token_logprob = picked - lse_roll
    return (new_state, divergence, token_logprob, roll_z, roll_x, roll_bc, roll_dt, roll_out)


def solution(mesh):
    return jax.shard_map(
        shards,
        mesh=mesh,
        in_specs=(
            P("group", None),
            P("group", "head", None, None),
            P("group", None, "head"),
            P("group", None, None),
            P("group"),
            P("group", "head"),
            P("group", "head"),
            P("group", "head"),
            P("group", None),
            P("group", "head"),
            P("group", "head"),
            P("head", "group"),
            P(None, "head"),
            P("head"),
            P(),
            P(),
            P("head"),
            P("head"),
            P("head"),
            P(),
            P("head"),
            P(),
        ),
        out_specs=(
            P("group", "head", None, None),
            P("group"),
            P("group"),
            P(None, "head"),
            P(None, "head"),
            P(),
            P(None, "head"),
            P(None, "head"),
        ),
        check_vma=False,
    )
```

profile of v0, /device:TPU:0, one launch (start us, length us, event | category | flops | bytes accessed | tf_op | source)
XLA Modules:
  0.0 324.4 jit_solution(13487269814347778549)
XLA Ops:
  7.2 0.7 all-gather.8.cloned.1.call-update
  7.9 0.7 all-gather.6.cloned.1.call-update
  8.7 0.7 all-gather.10.cloned.1.call-update
  10.0 10.6 %all_to_all.26 = bf16[8,800,320]{1,0,2:T(8,128)(2,1)} reshape(bf16[6400,320]{0,1:T(8,128)(2,1)} %param.33) | data formatting | bytes 8192000 | tf_op jit(solution)/shard_map/all_to_all | solution.py:84
  20.5 5.2 %copy.40 = bf16[8,800,320]{1,2,0:T(8,128)(2,1)} copy(bf16[8,800,320]{1,0,2:T(8,128)(2,1)} %all_to_all.26) | data formatting | bytes 8192000 | tf_op jit(solution)/shard_map/all_to_all | solution.py:84
  25.8 5.4 %all-to-all-start = ((bf16[8,800,320]{1,2,0:T(8,128)(2,1)}), bf16[8,800,320]{1,2,0:T(8,128)(2,1)}, u32[]{:S(2)}, u32[]{:S(2)}) async-start(bf16[8,800,320]{1,2,0:T(8,128)(2,1)} %copy.40), calls=%async_computation | async-start | bytes 9175040 | tf_op jit(solution)/shard_map/all_to_all | solution.py:84
  31.2 66.7 %all-gather = bf16[8,320,20]{1,2,0:T(8,128)(2,1)S(1)} all-gather(bf16[1,320,20]{1,2,0:T(8,128)(2,1)S(1)} %bitcast.39), channel_id=1, replica_groups=mesh['group'=8,'head'=4] {'group'}, dimensions={0}, use_global_device_ids=true | all-gather | bytes 115200 | tf_op jit(solution)/shard_map/all_gather | solution.py:47
  98.7 1.6 fusion.2
  100.4 16.8 %all-gather.6.cloned.1.call-done = bf16[2560,1280]{1,0:T(8,128)(2,1)} async-done(((bf16[320,1280]{1,0:T(8,128)(2,1)}), bf16[2560,1280]{1,0:T(8,128)(2,1)}) %all-gather.6.cloned.1.call-update) | async-done | bytes 6553616 | tf_op jit(solution)/shard_map/all_gather | solution.py:45
  117.2 3.9 %fusion.1 = bf16[16,1,1280]{2,0,1:T(8,128)(2,1)S(1)} fusion(bf16[2560,1280]{1,0:T(8,128)(2,1)} %all-gather.6.cloned.1.call-done, bf16[16,2560]{1,0:T(8,128)(2,1)S(1)} %copy-done.2, f32[2560]{0:T(1024)S(1)} %copy-done.6, f32[16]{0:T(128)S(1)} %add_rsqrt_fusion.2), kind=kOutput, calls=%fused_computation.4 | convolution fusion | flops 105041920 | bytes 6686784 | tf_op jit(solution)/shard_map/dot_general | solution.py:53
  121.3 8.4 %multiply_add_fusion = f32[16,20,64,128]{3,2,1,0:T(8,128)S(1)} fusion(f32[16,20,64,128]{3,2,1,0:T(8,128)} %param.23, f32[16,128]{1,0:T(8,128)S(1)} %get-tuple-element.19, f32[16,20,64]{2,1,0:T(8,128)S(1)} %broadcast_multiply_fusion, f32[16,20]{1,0:T(8,128)S(1)} %get-tuple-element.22), kind=kLoop, calls=%fused_computation | loop fusion | flops 7864320 | bytes 21062912 | tf_op jit(solution)/shard_map/add | solution.py:67
  129.8 4.1 %copy-done = f32[16,20,64,128]{3,2,1,0:T(8,128)} copy-done((f32[16,20,64,128]{3,2,1,0:T(8,128)}, f32[16,20,64,128]{3,2,1,0:T(8,128)S(1)}, u32[]{:S(2)}) %copy-start) | copy-done | bytes 10485784
  133.8 24.6 %fusion.21 = f32[16,1,20,64]{3,1,2,0:T(1,128)S(1)} fusion(f32[16,20,64,128]{3,2,1,0:T(8,128)S(1)} %multiply_add_fusion, f32[16,128,1,1]{1,2,3,0:T(1,128)S(1)} %bitcast.38), kind=kOutput, calls=%fused_computation.48 | convolution fusion | flops 31457280 | bytes 10575872 | tf_op jit(solution)/shard_map/shpn,sn->shp/dot_general | solution.py:68
  158.6 7.0 %all-gather.10.cloned.1.call-done = bf16[2560,1280]{1,0:T(8,128)(2,1)} async-done(((bf16[320,1280]{1,0:T(8,128)(2,1)}), bf16[2560,1280]{1,0:T(8,128)(2,1)}) %all-gather.10.cloned.1.call-update) | async-done | bytes 6553616 | tf_op jit(solution)/shard_map/all_gather | solution.py:44
  165.6 4.0 %multiply_reduce_fusion.2 = (f32[16]{0:T(128)S(1)}, f32[16,1280]{1,0:T(8,128)S(1)}) fusion(f32[16,1280]{1,0:T(8,128)S(1)} %reshape.100, bf16[2560,1280]{1,0:T(8,128)(2,1)} %all-gather.10.cloned.1.call-done, bf16[16,2560]{1,0:T(8,128)(2,1)S(1)} %copy-done.2, f32[2560]{0:T(1024)S(1)} %copy-done.6, f32[16]{0:T(128)S(1)} %add_rsqrt_fusion.2), kind=kOutput, calls=%fused_computation.31 | convolution fusion | flops 105205744 | bytes 6809728 | tf_op jit(solution)/shard_map/dot_general | solution.py:52
  169.6 11.7 %psum.42 = f32[16]{0:T(128)S(1)} all-reduce(f32[16]{0:T(128)S(1)} %get-tuple-element.24), channel_id=1, replica_groups=mesh['group'=8,'head'=4] {'head'}, use_global_device_ids=true, to_apply=%region_6.7 | all-reduce | flops 16 | bytes 128 | tf_op jit(solution)/shard_map/psum | solution.py:73
  181.3 32.6 %all-gather.12.cloned.1.call-done = bf16[2560,1280]{1,0:T(8,128)(2,1)} async-done(((bf16[320,1280]{1,0:T(8,128)(2,1)}), bf16[2560,1280]{1,0:T(8,128)(2,1)}) %all-gather.12.cloned.1.call-update) | async-done | bytes 6553616 | tf_op jit(solution)/shard_map/all_gather | solution.py:48
  213.9 5.4 %fusion.12 = f32[16,2560]{1,0:T(8,128)} fusion(bf16[2560,1280]{1,0:T(8,128)(2,1)} %all-gather.12.cloned.1.call-done, f32[16,1280]{1,0:T(8,128)S(1)} %get-tuple-element.25, f32[1280]{0:T(1024)S(1)} %copy-done.11, f32[16]{0:T(128)S(1)} %add_rsqrt_fusion.1), kind=kOutput, calls=%fused_computation.34 | convolution fusion | flops 104919040 | bytes 6804544 | tf_op jit(solution)/shard_map/dot_general | solution.py:78
  219.3 35.0 %all-reduce.4.cloned.1.call-done = f32[16,2560]{1,0:T(8,128)} async-done(((f32[16,2560]{1,0:T(8,128)}), f32[16,2560]{1,0:T(8,128)}) %all-reduce.4.cloned.1.call-update) | async-done | bytes 163856 | tf_op jit(solution)/shard_map/psum | solution.py:81
  254.3 1.0 multiply_reduce_fusion.1
  255.3 1.0 multiply_convert_fusion
  256.3 10.0 %all_gather.23 = bf16[128,2560]{1,0:T(8,128)(2,1)S(1)} all-gather(bf16[16,2560]{1,0:T(8,128)(2,1)S(1)} %multiply_convert_fusion), channel_id=1, replica_groups=mesh['group'=8,'head'=4] {'group'}, dimensions={0}, use_global_device_ids=true | all-gather | bytes 737280 | tf_op jit(solution)/shard_map/all_gather | solution.py:86
  266.4 3.9 %fusion.22 = f32[8,16,800]{2,1,0:T(8,128)} fusion(bf16[8,16,2560]{2,1,0:T(8,128)(2,1)S(1)} %bitcast.37, bf16[800,2560,1]{0,1,2:T(8,128)(2,1)} %bitcast.9), kind=kOutput, calls=%fused_computation.49 | convolution fusion | flops 524288000 | bytes 5160960 | tf_op jit(solution)/shard_map/dot_general | solution.py:85
  270.3 3.5 %all-to-all-start.1 = ((f32[8,16,800]{2,1,0:T(8,128)}), f32[8,16,800]{2,1,0:T(8,128)S(1)}, u32[]{:S(2)}, u32[]{:S(2)}) async-start(f32[8,16,800]{2,1,0:T(8,128)} %fusion.22), calls=%async_computation.1 | async-start | bytes 917504 | tf_op jit(solution)/shard_map/all_to_all | solution.py:91
  274.0 8.8 %all-to-all-done.1 = f32[8,16,800]{2,1,0:T(8,128)S(1)} async-done(((f32[8,16,800]{2,1,0:T(8,128)}), f32[8,16,800]{2,1,0:T(8,128)S(1)}, u32[]{:S(2)}, u32[]{:S(2)}) %all-to-all-start.1) | async-done | bytes 409632 | tf_op jit(solution)/shard_map/all_to_all | solution.py:91
  283.2 10.6 %all-reduce.1 = (f32[16]{0:T(128)S(1)}, f32[16]{0:T(128)S(1)}) all-reduce(bf16[16]{0:T(256)(128)(2,1)S(1)} %reduce_max.23, f32[16]{0:T(128)S(1)} %reduce_max.25), channel_id=1, replica_groups=mesh['group'=8,'head'=4] {'head'}, use_global_device_ids=true, to_apply=%region_4.5 | all-reduce | flops 32 | bytes 224 | tf_op jit(solution)/shard_map/pmax | solution.py:97
  294.5 8.5 %all-reduce = (f32[16]{0:T(128)S(1)}, f32[16]{0:T(128)S(1)}, f32[16]{0:T(128)S(1)}, f32[16]{0:T(128)S(1)}) all-reduce(f32[16]{0:T(128)S(1)} %get-tuple-element.11, f32[16]{0:T(128)S(1)} %get-tuple-element.10, f32[16]{0:T(128)S(1)} %get-tuple-element.9, f32[16]{0:T(128)S(1)} %get-tuple-element.8), channel_id=1, replica_groups=mesh['group'=8,'head'=4] {'head'}, use_global_device_ids=true, to_apply=%region_12.13 | all-reduce | flops 64 | bytes 512 | tf_op jit(solution)/shard_map/psum | solution.py:101
  303.0 0.5 fusion.15
  303.6 6.7 %copy.53 = bf16[2560,1280]{1,0:T(8,128)(2,1)} copy(bf16[2560,1280]{1,0:T(8,128)(2,1)} %all-gather.10.cloned.1.call-done) | data formatting | bytes 13107200
  310.3 3.3 %copy.54 = bf16[2560,1280]{1,0:T(8,128)(2,1)} copy(bf16[2560,1280]{1,0:T(8,128)(2,1)S(1)} %bitcast.33) | data formatting | bytes 13107200
  313.6 1.1 copy.55
  315.1 2.8 copy.56
  (80 shorter events, 3.7 us)
Async XLA Ops:
  7.2 91.5 %all-gather.8.cloned.1.call-start = ((), (), s32[]{:S(2)}) async-start(), calls=%async_computation.3 | async-start | bytes 1474560 | tf_op jit(solution)/shard_map/all_gather | solution.py:46
  7.9 109.3 %all-gather.6.cloned.1.call-start = ((), (), s32[]{:S(2)}) async-start(), calls=%async_computation.2 | async-start | bytes 7372800 | tf_op jit(solution)/shard_map/all_gather | solution.py:45
  8.7 157.0 %all-gather.10.cloned.1.call-start = ((), (), s32[]{:S(2)}) async-start(), calls=%async_computation.4 | async-start | bytes 7372800 | tf_op jit(solution)/shard_map/all_gather | solution.py:44
  9.4 204.5 %all-gather.12.cloned.1.call-start = ((), (), s32[]{:S(2)}) async-start(), calls=%async_computation.5 | async-start | bytes 7372800 | tf_op jit(solution)/shard_map/all_gather | solution.py:48
  25.7 5.5 %copy-start.9 = (bf16[320,20]{0,1:T(8,128)(2,1)S(1)}, bf16[320,20]{0,1:T(8,128)(2,1)}, u32[]{:S(2)}) copy-start(bf16[320,20]{0,1:T(8,128)(2,1)} %param.31) | copy-start | bytes 38404
  25.7 72.4 %copy-start.17 = (f32[20]{0:T(128)S(1)}, f32[20]{0:T(128)}, u32[]{:S(2)}) copy-start(f32[20]{0:T(128)} %param.39) | copy-start | bytes 244
  25.7 72.4 %copy-start.12 = (f32[1280]{0:T(1024)S(1)}, f32[1280]{0:T(1024)}, u32[]{:S(2)}) copy-start(f32[1280]{0:T(1024)} %param.35) | copy-start | bytes 15364
  25.7 72.5 %copy-start.2 = (bf16[16,2560]{1,0:T(8,128)(2,1)S(1)}, bf16[16,2560]{1,0:T(8,128)(2,1)}, u32[]{:S(2)}) copy-start(bf16[16,2560]{1,0:T(8,128)(2,1)} %param.22) | copy-start | bytes 245764
  25.7 72.6 %copy-start.6 = (f32[2560]{0:T(1024)S(1)}, f32[2560]{0:T(1024)}, u32[]{:S(2)}) copy-start(f32[2560]{0:T(1024)} %param.41) | copy-start | bytes 30724
  25.7 72.6 %copy-start.18 = (f32[20]{0:T(128)S(1)}, f32[20]{0:T(128)}, u32[]{:S(2)}) copy-start(f32[20]{0:T(128)} %param.38) | copy-start | bytes 244
  25.8 74.5 %copy-start.7 = (bf16[16,3,256]{2,0,1:T(8,128)(2,1)S(1)}, bf16[16,3,256]{2,0,1:T(8,128)(2,1)}, u32[]{:S(2)}) copy-start(bf16[16,3,256]{2,0,1:T(8,128)(2,1)} %param.25) | copy-start | bytes 73732
  25.8 74.5 %copy-start.13 = (f32[4,256]{1,0:T(4,128)S(1)}, f32[4,256]{1,0:T(4,128)}, u32[]{:S(2)}) copy-start(f32[4,256]{1,0:T(4,128)} %param.36) | copy-start | bytes 12292
  25.8 74.5 %copy-start.14 = (f32[256]{0:T(256)S(1)}, f32[256]{0:T(256)}, u32[]{:S(2)}) copy-start(f32[256]{0:T(256)} %param.37) | copy-start | bytes 3076
  25.8 240.6 %all-to-all-start = ((bf16[8,800,320]{1,2,0:T(8,128)(2,1)}), bf16[8,800,320]{1,2,0:T(8,128)(2,1)}, u32[]{:S(2)}, u32[]{:S(2)}) async-start(bf16[8,800,320]{1,2,0:T(8,128)(2,1)} %copy.40), calls=%async_computation | async-start | bytes 9175040 | tf_op jit(solution)/shard_map/all_to_all | solution.py:84
  31.2 89.9 %copy-start.4 = (bf16[16,3,1280]{2,0,1:T(8,128)(2,1)S(1)}, bf16[16,3,1280]{2,0,1:T(8,128)(2,1)}, u32[]{:S(2)}) copy-start(bf16[16,3,1280]{2,0,1:T(8,128)(2,1)} %param.24) | copy-start | bytes 368644
  31.2 89.9 %copy-start.8 = (f32[4,1280]{1,0:T(4,128)S(1)}, f32[4,1280]{1,0:T(4,128)}, u32[]{:S(2)}) copy-start(f32[4,1280]{1,0:T(4,128)} %param.34) | copy-start | bytes 61444
  31.2 223.1 %all-reduce.4.cloned.1.call-start = ((), (), s32[]{:S(2)}) async-start(), calls=%async_computation.6 | async-start | bytes 327680 | tf_op jit(solution)/shard_map/psum | solution.py:81
  98.1 31.6 %copy-start.5 = (bf16[2560,20]{0,1:T(8,128)(2,1)}, bf16[2560,20]{0,1:T(8,128)(2,1)S(1)}, u32[]{:S(2)}) copy-start(bf16[2560,20]{0,1:T(8,128)(2,1)S(1)} %reshape.102) | copy-start | bytes 307204
  129.7 4.1 %copy-start = (f32[16,20,64,128]{3,2,1,0:T(8,128)}, f32[16,20,64,128]{3,2,1,0:T(8,128)S(1)}, u32[]{:S(2)}) copy-start(f32[16,20,64,128]{3,2,1,0:T(8,128)S(1)} %multiply_add_fusion) | copy-start | bytes 31457284
  129.8 28.7 %copy-start.15 = (f32[20]{0:T(128)S(1)}, f32[20]{0:T(128)}, u32[]{:S(2)}) copy-start(f32[20]{0:T(128)} %param.40) | copy-start | bytes 244
  133.8 80.1 %copy-start.11 = (f32[1280]{0:T(1024)S(1)}, f32[1280]{0:T(1024)}, u32[]{:S(2)}) copy-start(f32[1280]{0:T(1024)} %param.42) | copy-start | bytes 15364
  158.6 96.7 %copy-start.10 = (f32[2560]{0:T(1024)S(1)}, f32[2560]{0:T(1024)}, u32[]{:S(2)}) copy-start(f32[2560]{0:T(1024)} %param.43) | copy-start | bytes 30724
  213.9 59.9 %copy-start.3 = (bf16[16,6400]{1,0:T(8,128)(2,1)S(1)}, bf16[16,6400]{1,0:T(8,128)(2,1)}, u32[]{:S(2)}) copy-start(bf16[16,6400]{1,0:T(8,128)(2,1)} %param.27) | copy-start | bytes 614404
  219.3 74.9 %copy-start.16 = (s32[16]{0:T(128)S(1)}, s32[16]{0:T(128)}, u32[]{:S(2)}) copy-start(s32[16]{0:T(128)} %param.26) | copy-start | bytes 196
  270.3 12.4 %all-to-all-start.1 = ((f32[8,16,800]{2,1,0:T(8,128)}), f32[8,16,800]{2,1,0:T(8,128)S(1)}, u32[]{:S(2)}, u32[]{:S(2)}) async-start(f32[8,16,800]{2,1,0:T(8,128)} %fusion.22), calls=%async_computation.1 | async-start | bytes 917504 | tf_op jit(solution)/shard_map/all_to_all | solution.py:91
  293.9 16.4 %slice-start = ((s8[6553600]{0:T(1024)(128)(4,1)}), s8[2359296]{0:T(1024)(128)(4,1)S(1)}, s32[]{:S(2)}) async-start(s8[6553600]{0:T(1024)(128)(4,1)} %bitcast.32), calls=%async_computation.7 | async-start | bytes 4718592
  303.6 6.7 %slice-start.1 = ((s8[6553600]{0:T(1024)(128)(4,1)}), s8[4194304]{0:T(1024)(128)(4,1)S(1)}, s32[]{:S(2)}) async-start(s8[6553600]{0:T(1024)(128)(4,1)} %bitcast.32), calls=%async_computation.8 | async-start | bytes 8388608
  303.6 11.1 %slice-start.2 = ((s8[6553600]{0:T(1024)(128)(4,1)}), s8[4194304]{0:T(1024)(128)(4,1)S(1)}, s32[]{:S(2)}) async-start(s8[6553600]{0:T(1024)(128)(4,1)} %bitcast.34), calls=%async_computation.9 | async-start | bytes 8388608
  310.3 3.3 %copy-start.1 = (bf16[2560,256]{1,0:T(8,128)(2,1)S(1)}, bf16[2560,256]{1,0:T(8,128)(2,1)}, u32[]{:S(2)}) copy-start(bf16[2560,256]{1,0:T(8,128)(2,1)} %all-gather.8.cloned.1.call-done) | copy-start | bytes 3932164
  310.3 4.8 %slice-start.3 = ((s8[6553600]{0:T(1024)(128)(4,1)}), s8[2359296]{0:T(1024)(128)(4,1)S(1)}, s32[]{:S(2)}) async-start(s8[6553600]{0:T(1024)(128)(4,1)} %bitcast.34), calls=%async_computation.10 | async-start | bytes 4718592
Sparse Core Ops, SparseCore 0:
  9.9 28.3 all-gather.7
  40.1 77.0 all-gather.5
  119.1 46.4 all-gather.9
  167.4 46.4 all-gather.11
  219.4 34.8 all-reduce.3
where the time goes:
time: 325 us; the launch traced here: 324 us
  blocking collectives  108 us (33%)
  waiting for transfers between devices  103 us (32%)
  matrix products  43.6 us (13%)
  local copies, waits for them, and re-layouts  34.9 us (11%)
  between operations  14.1 us (4%)
  other arithmetic  12.4 us (4%)
  starting transfers between devices  9.02 us (3%)
    all_gather x1, blocking collectives, shards(): lax.all_gather(in_dt, 'group', axis=0, tiled=True)  66.7 us
    psum x1, waiting for transfers between devices, shards(): mixed = lax.psum(partial_mix, 'head')  35 us
    all_gather x1, waiting for transfers between devices, shards(): lax.all_gather(out_t, 'group', axis=0, tiled=True)  32.6 us
    dot_general x1, matrix products, shards(): jnp.einsum('shpn,sn->shp', new_state, c_vals, precision=lax.Precision.HIG...  24.6 us
    unnamed x51, local copies, waits for them, and re-layouts  18.6 us
    all_gather x1, waiting for transfers between devices, shards(): lax.all_gather(in_x, 'group', axis=0, tiled=True)  16.8 us
    all_to_all x2, local copies, waits for them, and re-layouts, shards(): lax.all_to_all(lm_head, 'group', split_axis=0, concat_axis=1, tiled=True)  15.8 us
    psum x1, blocking collectives, shards(): square_total = lax.psum(jnp.sum(gated * gated, axis=-1), 'head')  11.7 us
  transfers between devices with their start and end apart: 7, of which 5 were waited for; matrix products, arithmetic and copies ran while one was open for 17% of the time, Pallas kernels for 0%

commit v1 on v0

--- a/solution.py
+++ b/solution.py
@@ -78,7 +78,8 @@
     partial_mix = lax.dot_general(
         gated_out, roll_out, (((1,), (1,)), ((), ())), preferred_element_type=jnp.float32
     )
-    mixed = lax.psum(partial_mix, "head")
+    parts = lax.all_gather(partial_mix, "head", axis=0, tiled=False)
+    mixed = parts.sum(axis=0)
     final_hidden = rms_norm(stream_in + mixed, final_gain).astype(jnp.bfloat16)
     vocab_local = lm_head.shape[0]
     whole_rows = lax.all_to_all(lm_head, "group", split_axis=0, concat_axis=1, tiled=True)

time: 325 us -> 306 us (0.942)
  waiting for transfers between devices: 103 us -> 67.8 us
  blocking collectives: 108 us -> 126 us
    psum x1 -> x0, waiting for transfers between devices: 35 us -> none  [shards(): mixed = lax.psum(partial_mix, 'head')]
    all_gather x0 -> x1, blocking collectives: none -> 18.3 us  [shards(): parts = lax.all_gather(partial_mix, 'head', axis=0, tiled=False)]
  transfers between devices with their start and end apart: 7 -> 6, of which waited for: 5 -> 4; matrix products, arithmetic and copies ran while one was open for 17% -> 18% of each run, Pallas kernels for 0% -> 0%
where the time goes in v1:
time: 306 us; the launch traced here: 305 us
  blocking collectives  126 us (41%)
  waiting for transfers between devices  67.8 us (22%)
  matrix products  42.9 us (14%)
  local copies, waits for them, and re-layouts  34.9 us (11%)
  between operations  14.1 us (5%)
  other arithmetic  10.6 us (3%)
  starting transfers between devices  8.98 us (3%)
    all_gather x1, blocking collectives, shards(): lax.all_gather(in_dt, 'group', axis=0, tiled=True)  66.8 us
    all_gather x1, waiting for transfers between devices, shards(): lax.all_gather(out_t, 'group', axis=0, tiled=True)  32.6 us
    dot_general x1, matrix products, shards(): jnp.einsum('shpn,sn->shp', new_state, c_vals, precision=lax.Precision.HIG...  24.6 us
    unnamed x51, local copies, waits for them, and re-layouts  18.6 us
    all_gather x1, blocking collectives, shards(): parts = lax.all_gather(partial_mix, 'head', axis=0, tiled=False)  18.3 us
    all_gather x1, waiting for transfers between devices, shards(): lax.all_gather(in_x, 'group', axis=0, tiled=True)  16.8 us
    all_to_all x2, local copies, waits for them, and re-layouts, shards(): lax.all_to_all(lm_head, 'group', split_axis=0, concat_axis=1, tiled=True)  15.8 us
    psum x1, blocking collectives, shards(): square_total = lax.psum(jnp.sum(gated * gated, axis=-1), 'head')  11.7 us
  transfers between devices with their start and end apart: 6, of which 4 were waited for; matrix products, arithmetic and copies ran while one was open for 18% of the time, Pallas kernels for 0%

profile of v1, /device:TPU:0, one launch (start us, length us, event | category | flops | bytes accessed | tf_op | source)
XLA Modules:
  0.0 305.5 jit_solution(9979581910576380910)
XLA Ops:
  7.2 0.7 all-gather.9.cloned.1.call-update
  7.9 0.7 all-gather.7.cloned.1.call-update
  8.7 0.7 all-gather.11.cloned.1.call-update
  9.4 0.5 all-gather.13.cloned.1.call-update
  10.0 10.6 %all_to_all.26 = bf16[8,800,320]{1,0,2:T(8,128)(2,1)} reshape(bf16[6400,320]{0,1:T(8,128)(2,1)} %param.33) | data formatting | bytes 8192000 | tf_op jit(solution)/shard_map/all_to_all | solution.py:85
  20.5 5.2 %copy.40 = bf16[8,800,320]{1,2,0:T(8,128)(2,1)} copy(bf16[8,800,320]{1,0,2:T(8,128)(2,1)} %all_to_all.26) | data formatting | bytes 8192000 | tf_op jit(solution)/shard_map/all_to_all | solution.py:85
  25.8 5.4 %all-to-all-start = ((bf16[8,800,320]{1,2,0:T(8,128)(2,1)}), bf16[8,800,320]{1,2,0:T(8,128)(2,1)}, u32[]{:S(2)}, u32[]{:S(2)}) async-start(bf16[8,800,320]{1,2,0:T(8,128)(2,1)} %copy.40), calls=%async_computation | async-start | bytes 9175040 | tf_op jit(solution)/shard_map/all_to_all | solution.py:85
  31.2 66.8 %all-gather.1 = bf16[8,320,20]{1,2,0:T(8,128)(2,1)S(1)} all-gather(bf16[1,320,20]{1,2,0:T(8,128)(2,1)S(1)} %bitcast.41), channel_id=1, replica_groups=mesh['group'=8,'head'=4] {'group'}, dimensions={0}, use_global_device_ids=true | all-gather | bytes 115200 | tf_op jit(solution)/shard_map/all_gather | solution.py:47
  98.7 1.6 fusion.2
  100.4 16.8 %all-gather.7.cloned.1.call-done = bf16[2560,1280]{1,0:T(8,128)(2,1)} async-done(((bf16[320,1280]{1,0:T(8,128)(2,1)}), bf16[2560,1280]{1,0:T(8,128)(2,1)}) %all-gather.7.cloned.1.call-update) | async-done | bytes 6553616 | tf_op jit(solution)/shard_map/all_gather | solution.py:45
  117.2 3.9 %fusion.1 = bf16[16,1,1280]{2,0,1:T(8,128)(2,1)S(1)} fusion(bf16[2560,1280]{1,0:T(8,128)(2,1)} %all-gather.7.cloned.1.call-done, bf16[16,2560]{1,0:T(8,128)(2,1)S(1)} %copy-done.2, f32[2560]{0:T(1024)S(1)} %copy-done.6, f32[16]{0:T(128)S(1)} %add_rsqrt_fusion.2), kind=kOutput, calls=%fused_computation.4 | convolution fusion | flops 105041920 | bytes 6686784 | tf_op jit(solution)/shard_map/dot_general | solution.py:53
  121.3 8.4 %multiply_add_fusion = f32[16,20,64,128]{3,2,1,0:T(8,128)S(1)} fusion(f32[16,20,64,128]{3,2,1,0:T(8,128)} %param.23, f32[16,128]{1,0:T(8,128)S(1)} %get-tuple-element.19, f32[16,20,64]{2,1,0:T(8,128)S(1)} %broadcast_multiply_fusion, f32[16,20]{1,0:T(8,128)S(1)} %get-tuple-element.22), kind=kLoop, calls=%fused_computation | loop fusion | flops 7864320 | bytes 21062912 | tf_op jit(solution)/shard_map/add | solution.py:67
  129.8 4.1 %copy-done = f32[16,20,64,128]{3,2,1,0:T(8,128)} copy-done((f32[16,20,64,128]{3,2,1,0:T(8,128)}, f32[16,20,64,128]{3,2,1,0:T(8,128)S(1)}, u32[]{:S(2)}) %copy-start) | copy-done | bytes 10485784
  133.8 24.6 %fusion.21 = f32[16,1,20,64]{3,1,2,0:T(1,128)S(1)} fusion(f32[16,20,64,128]{3,2,1,0:T(8,128)S(1)} %multiply_add_fusion, f32[16,128,1,1]{1,2,3,0:T(1,128)S(1)} %bitcast.40), kind=kOutput, calls=%fused_computation.48 | convolution fusion | flops 31457280 | bytes 10575872 | tf_op jit(solution)/shard_map/shpn,sn->shp/dot_general | solution.py:68
  158.6 7.0 %all-gather.11.cloned.1.call-done = bf16[2560,1280]{1,0:T(8,128)(2,1)} async-done(((bf16[320,1280]{1,0:T(8,128)(2,1)}), bf16[2560,1280]{1,0:T(8,128)(2,1)}) %all-gather.11.cloned.1.call-update) | async-done | bytes 6553616 | tf_op jit(solution)/shard_map/all_gather | solution.py:44
  165.6 4.0 %multiply_reduce_fusion.2 = (f32[16]{0:T(128)S(1)}, f32[16,1280]{1,0:T(8,128)S(1)}) fusion(f32[16,1280]{1,0:T(8,128)S(1)} %reshape.100, bf16[2560,1280]{1,0:T(8,128)(2,1)} %all-gather.11.cloned.1.call-done, bf16[16,2560]{1,0:T(8,128)(2,1)S(1)} %copy-done.2, f32[2560]{0:T(1024)S(1)} %copy-done.6, f32[16]{0:T(128)S(1)} %add_rsqrt_fusion.2), kind=kOutput, calls=%fused_computation.31 | convolution fusion | flops 105205744 | bytes 6809728 | tf_op jit(solution)/shard_map/dot_general | solution.py:52
  169.6 11.7 %psum.35 = f32[16]{0:T(128)S(1)} all-reduce(f32[16]{0:T(128)S(1)} %get-tuple-element.24), channel_id=1, replica_groups=mesh['group'=8,'head'=4] {'head'}, use_global_device_ids=true, to_apply=%region_6.7 | all-reduce | flops 16 | bytes 128 | tf_op jit(solution)/shard_map/psum | solution.py:73
  181.3 32.6 %all-gather.13.cloned.1.call-done = bf16[2560,1280]{1,0:T(8,128)(2,1)} async-done(((bf16[320,1280]{1,0:T(8,128)(2,1)}), bf16[2560,1280]{1,0:T(8,128)(2,1)}) %all-gather.13.cloned.1.call-update) | async-done | bytes 6553616 | tf_op jit(solution)/shard_map/all_gather | solution.py:48
  213.9 4.7 %fusion.12 = f32[16,2560]{1,0:T(8,128)S(1)} fusion(bf16[2560,1280]{1,0:T(8,128)(2,1)} %all-gather.13.cloned.1.call-done, f32[16,1280]{1,0:T(8,128)S(1)} %get-tuple-element.25, f32[1280]{0:T(1024)S(1)} %copy-done.11, f32[16]{0:T(128)S(1)} %add_rsqrt_fusion.1), kind=kOutput, calls=%fused_computation.34 | convolution fusion | flops 104919040 | bytes 6804544 | tf_op jit(solution)/shard_map/dot_general | solution.py:78
  218.5 18.3 %all-gather = f32[64,2560]{1,0:T(8,128)S(1)} all-gather(f32[16,2560]{1,0:T(8,128)S(1)} %fusion.12), channel_id=2, replica_groups=mesh['group'=8,'head'=4] {'head'}, dimensions={0}, use_global_device_ids=true | all-gather | bytes 819200 | tf_op jit(solution)/shard_map/all_gather | solution.py:81
  237.1 10.1 %all_gather.31 = bf16[128,2560]{1,0:T(8,128)(2,1)S(1)} all-gather(bf16[16,2560]{1,0:T(8,128)(2,1)S(1)} %multiply_convert_fusion), channel_id=1, replica_groups=mesh['group'=8,'head'=4] {'group'}, dimensions={0}, use_global_device_ids=true | all-gather | bytes 737280 | tf_op jit(solution)/shard_map/all_gather | solution.py:87
  247.2 3.9 %fusion.22 = f32[8,16,800]{2,1,0:T(8,128)} fusion(bf16[8,16,2560]{2,1,0:T(8,128)(2,1)S(1)} %bitcast.38, bf16[800,2560,1]{0,1,2:T(8,128)(2,1)} %bitcast.10), kind=kOutput, calls=%fused_computation.49 | convolution fusion | flops 524288000 | bytes 5160960 | tf_op jit(solution)/shard_map/dot_general | solution.py:86
  251.1 3.5 %all-to-all-start.1 = ((f32[8,16,800]{2,1,0:T(8,128)}), f32[8,16,800]{2,1,0:T(8,128)S(1)}, u32[]{:S(2)}, u32[]{:S(2)}) async-start(f32[8,16,800]{2,1,0:T(8,128)} %fusion.22), calls=%async_computation.1 | async-start | bytes 917504 | tf_op jit(solution)/shard_map/all_to_all | solution.py:92
  254.8 8.8 %all-to-all-done.1 = f32[8,16,800]{2,1,0:T(8,128)S(1)} async-done(((f32[8,16,800]{2,1,0:T(8,128)}), f32[8,16,800]{2,1,0:T(8,128)S(1)}, u32[]{:S(2)}, u32[]{:S(2)}) %all-to-all-start.1) | async-done | bytes 409632 | tf_op jit(solution)/shard_map/all_to_all | solution.py:92
  264.0 10.9 %all-reduce.1 = (f32[16]{0:T(128)S(1)}, f32[16]{0:T(128)S(1)}) all-reduce(bf16[16]{0:T(256)(128)(2,1)S(1)} %reduce_max.23, f32[16]{0:T(128)S(1)} %reduce_max.25), channel_id=1, replica_groups=mesh['group'=8,'head'=4] {'head'}, use_global_device_ids=true, to_apply=%region_4.5 | all-reduce | flops 32 | bytes 224 | tf_op jit(solution)/shard_map/pmax | solution.py:98
  275.6 8.5 %all-reduce = (f32[16]{0:T(128)S(1)}, f32[16]{0:T(128)S(1)}, f32[16]{0:T(128)S(1)}, f32[16]{0:T(128)S(1)}) all-reduce(f32[16]{0:T(128)S(1)} %get-tuple-element.11, f32[16]{0:T(128)S(1)} %get-tuple-element.10, f32[16]{0:T(128)S(1)} %get-tuple-element.9, f32[16]{0:T(128)S(1)} %get-tuple-element.8), channel_id=1, replica_groups=mesh['group'=8,'head'=4] {'head'}, use_global_device_ids=true, to_apply=%region_12.13 | all-reduce | flops 64 | bytes 512 | tf_op jit(solution)/shard_map/psum | solution.py:102
  284.1 0.5 fusion.15
  284.6 6.7 %copy.52 = bf16[2560,1280]{1,0:T(8,128)(2,1)} copy(bf16[2560,1280]{1,0:T(8,128)(2,1)} %all-gather.11.cloned.1.call-done) | data formatting | bytes 13107200
  291.3 3.3 %copy.53 = bf16[2560,1280]{1,0:T(8,128)(2,1)} copy(bf16[2560,1280]{1,0:T(8,128)(2,1)S(1)} %bitcast.34) | data formatting | bytes 13107200
  294.7 1.1 copy.54
  295.7 0.4 slice-done.3
  296.1 2.8 copy.55
  (79 shorter events, 3.0 us)
Async XLA Ops:
  7.2 91.5 %all-gather.9.cloned.1.call-start = ((), (), s32[]{:S(2)}) async-start(), calls=%async_computation.3 | async-start | bytes 1474560 | tf_op jit(solution)/shard_map/all_gather | solution.py:46
  7.9 109.3 %all-gather.7.cloned.1.call-start = ((), (), s32[]{:S(2)}) async-start(), calls=%async_computation.2 | async-start | bytes 7372800 | tf_op jit(solution)/shard_map/all_gather | solution.py:45
  8.7 157.0 %all-gather.11.cloned.1.call-start = ((), (), s32[]{:S(2)}) async-start(), calls=%async_computation.4 | async-start | bytes 7372800 | tf_op jit(solution)/shard_map/all_gather | solution.py:44
  9.4 204.5 %all-gather.13.cloned.1.call-start = ((), (), s32[]{:S(2)}) async-start(), calls=%async_computation.5 | async-start | bytes 7372800 | tf_op jit(solution)/shard_map/all_gather | solution.py:48
  25.7 5.4 %copy-start.9 = (bf16[320,20]{0,1:T(8,128)(2,1)S(1)}, bf16[320,20]{0,1:T(8,128)(2,1)}, u32[]{:S(2)}) copy-start(bf16[320,20]{0,1:T(8,128)(2,1)} %param.31) | copy-start | bytes 38404
  25.7 72.4 %copy-start.17 = (f32[20]{0:T(128)S(1)}, f32[20]{0:T(128)}, u32[]{:S(2)}) copy-start(f32[20]{0:T(128)} %param.39) | copy-start | bytes 244
  25.7 72.4 %copy-start.12 = (f32[1280]{0:T(1024)S(1)}, f32[1280]{0:T(1024)}, u32[]{:S(2)}) copy-start(f32[1280]{0:T(1024)} %param.35) | copy-start | bytes 15364
  25.7 72.5 %copy-start.2 = (bf16[16,2560]{1,0:T(8,128)(2,1)S(1)}, bf16[16,2560]{1,0:T(8,128)(2,1)}, u32[]{:S(2)}) copy-start(bf16[16,2560]{1,0:T(8,128)(2,1)} %param.22) | copy-start | bytes 245764
  25.7 72.6 %copy-start.6 = (f32[2560]{0:T(1024)S(1)}, f32[2560]{0:T(1024)}, u32[]{:S(2)}) copy-start(f32[2560]{0:T(1024)} %param.41) | copy-start | bytes 30724
  25.7 72.6 %copy-start.18 = (f32[20]{0:T(128)S(1)}, f32[20]{0:T(128)}, u32[]{:S(2)}) copy-start(f32[20]{0:T(128)} %param.38) | copy-start | bytes 244
  25.8 74.5 %copy-start.7 = (bf16[16,3,256]{2,0,1:T(8,128)(2,1)S(1)}, bf16[16,3,256]{2,0,1:T(8,128)(2,1)}, u32[]{:S(2)}) copy-start(bf16[16,3,256]{2,0,1:T(8,128)(2,1)} %param.25) | copy-start | bytes 73732
  25.8 74.5 %copy-start.13 = (f32[4,256]{1,0:T(4,128)S(1)}, f32[4,256]{1,0:T(4,128)}, u32[]{:S(2)}) copy-start(f32[4,256]{1,0:T(4,128)} %param.36) | copy-start | bytes 12292
  25.8 74.5 %copy-start.14 = (f32[256]{0:T(256)S(1)}, f32[256]{0:T(256)}, u32[]{:S(2)}) copy-start(f32[256]{0:T(256)} %param.37) | copy-start | bytes 3076
  25.8 221.4 %all-to-all-start = ((bf16[8,800,320]{1,2,0:T(8,128)(2,1)}), bf16[8,800,320]{1,2,0:T(8,128)(2,1)}, u32[]{:S(2)}, u32[]{:S(2)}) async-start(bf16[8,800,320]{1,2,0:T(8,128)(2,1)} %copy.40), calls=%async_computation | async-start | bytes 9175040 | tf_op jit(solution)/shard_map/all_to_all | solution.py:85
  31.2 89.9 %copy-start.4 = (bf16[16,3,1280]{2,0,1:T(8,128)(2,1)S(1)}, bf16[16,3,1280]{2,0,1:T(8,128)(2,1)}, u32[]{:S(2)}) copy-start(bf16[16,3,1280]{2,0,1:T(8,128)(2,1)} %param.24) | copy-start | bytes 368644
  31.2 89.9 %copy-start.8 = (f32[4,1280]{1,0:T(4,128)S(1)}, f32[4,1280]{1,0:T(4,128)}, u32[]{:S(2)}) copy-start(f32[4,1280]{1,0:T(4,128)} %param.34) | copy-start | bytes 61444
  98.1 31.6 %copy-start.5 = (bf16[2560,20]{0,1:T(8,128)(2,1)}, bf16[2560,20]{0,1:T(8,128)(2,1)S(1)}, u32[]{:S(2)}) copy-start(bf16[2560,20]{0,1:T(8,128)(2,1)S(1)} %reshape.103) | copy-start | bytes 307204
  129.7 4.1 %copy-start = (f32[16,20,64,128]{3,2,1,0:T(8,128)}, f32[16,20,64,128]{3,2,1,0:T(8,128)S(1)}, u32[]{:S(2)}) copy-start(f32[16,20,64,128]{3,2,1,0:T(8,128)S(1)} %multiply_add_fusion) | copy-start | bytes 31457284
  129.8 28.7 %copy-start.15 = (f32[20]{0:T(128)S(1)}, f32[20]{0:T(128)}, u32[]{:S(2)}) copy-start(f32[20]{0:T(128)} %param.40) | copy-start | bytes 244
  133.8 80.1 %copy-start.11 = (f32[1280]{0:T(1024)S(1)}, f32[1280]{0:T(1024)}, u32[]{:S(2)}) copy-start(f32[1280]{0:T(1024)} %param.42) | copy-start | bytes 15364
  158.6 78.4 %copy-start.10 = (f32[2560]{0:T(1024)S(1)}, f32[2560]{0:T(1024)}, u32[]{:S(2)}) copy-start(f32[2560]{0:T(1024)} %param.43) | copy-start | bytes 30724
  218.5 36.0 %copy-start.3 = (bf16[16,6400]{1,0:T(8,128)(2,1)S(1)}, bf16[16,6400]{1,0:T(8,128)(2,1)}, u32[]{:S(2)}) copy-start(bf16[16,6400]{1,0:T(8,128)(2,1)} %param.27) | copy-start | bytes 614404
  236.8 38.5 %copy-start.16 = (s32[16]{0:T(128)S(1)}, s32[16]{0:T(128)}, u32[]{:S(2)}) copy-start(s32[16]{0:T(128)} %param.26) | copy-start | bytes 196
  251.1 12.4 %all-to-all-start.1 = ((f32[8,16,800]{2,1,0:T(8,128)}), f32[8,16,800]{2,1,0:T(8,128)S(1)}, u32[]{:S(2)}, u32[]{:S(2)}) async-start(f32[8,16,800]{2,1,0:T(8,128)} %fusion.22), calls=%async_computation.1 | async-start | bytes 917504 | tf_op jit(solution)/shard_map/all_to_all | solution.py:92
  274.9 16.4 %slice-start = ((s8[6553600]{0:T(1024)(128)(4,1)}), s8[2359296]{0:T(1024)(128)(4,1)S(1)}, s32[]{:S(2)}) async-start(s8[6553600]{0:T(1024)(128)(4,1)} %bitcast.33), calls=%async_computation.6 | async-start | bytes 4718592
  284.6 6.7 %slice-start.1 = ((s8[6553600]{0:T(1024)(128)(4,1)}), s8[4194304]{0:T(1024)(128)(4,1)S(1)}, s32[]{:S(2)}) async-start(s8[6553600]{0:T(1024)(128)(4,1)} %bitcast.33), calls=%async_computation.7 | async-start | bytes 8388608
  284.6 11.1 %slice-start.2 = ((s8[6553600]{0:T(1024)(128)(4,1)}), s8[4194304]{0:T(1024)(128)(4,1)S(1)}, s32[]{:S(2)}) async-start(s8[6553600]{0:T(1024)(128)(4,1)} %bitcast.35), calls=%async_computation.8 | async-start | bytes 8388608
  291.3 3.3 %copy-start.1 = (bf16[2560,256]{1,0:T(8,128)(2,1)S(1)}, bf16[2560,256]{1,0:T(8,128)(2,1)}, u32[]{:S(2)}) copy-start(bf16[2560,256]{1,0:T(8,128)(2,1)} %all-gather.9.cloned.1.call-done) | copy-start | bytes 3932164
  291.3 4.8 %slice-start.3 = ((s8[6553600]{0:T(1024)(128)(4,1)}), s8[2359296]{0:T(1024)(128)(4,1)S(1)}, s32[]{:S(2)}) async-start(s8[6553600]{0:T(1024)(128)(4,1)} %bitcast.35), calls=%async_computation.9 | async-start | bytes 4718592
Sparse Core Ops, SparseCore 0:
  9.9 28.3 all-gather.8
  40.1 77.0 all-gather.6
  119.1 46.4 all-gather.10
  167.4 46.4 all-gather.12
